TPU v7x, 256 devices: a 2x2x32 block of a 4x8x32 slice. The times are simulated.
256 devices in a mesh: groups: 4 (over x, y), feat: 64 (over z, core).
Axes of the slice: x: 2, y: 2, z: 32, core: 2. Of those that a mesh axis runs over, the one named last changes fastest.
The devices are a block of a 4x8x32 slice.
Arguments:
- cells: bfloat16 [768, 512, 192], P('groups', 'feat'), parts along dimension 0, may hold values from -6 to 6
- missing: int32 [768, 512], P('groups', 'feat'), parts along dimension 0, may hold values 0 or 1
- feat_ids: int32 [2048], P(('groups', 'feat')), parts along dimension 0, may hold values from 0 to 63
- feat_table: float32 [64, 192], replicated, may hold values from -5 to 5
- nan_embed: float32 [192], replicated, may hold values from -5 to 5
- gain_one: float32 [192], replicated, may hold values from 0.1 to 1.9
- w_qkv: bfloat16 [192, 576], replicated, may hold values from -3 to 3
- w_out: bfloat16 [192, 192], replicated, may hold values from -0.4375 to 0.4375
- gain_two: float32 [192], replicated, may hold values from 0.1 to 1.9
- w_up: bfloat16 [192, 768], replicated, may hold values from -0.4375 to 0.4375
- w_down: bfloat16 [768, 192], replicated, may hold values from -0.21875 to 0.21875
Outputs:
- result: float32 [768, 512, 192], P('groups', 'feat'), parts along dimension 0
There are 4 independent parts, one for each index of `groups`. A program takes and returns all parts, laid end to end along the dimension named above; an argument that names none is the same for every part. Nothing has to cross between parts.
All inputs are finite; a program needn't handle non-finite values. No bound on the sum of `missing` on one device may be relied on, other than what follows from the above.
Results may differ from a plain program's by a relative error of at most 0.007.
The roundings to bfloat16 on the way count: a program that leaves them out, or rounds other values in their place, can miss the bound.
Values may be sent and summed in bfloat16 or wider, within the bound.
A program may use at most 64 MiB of HBM per device.

v0:
```python
import jax
import jax.numpy as jnp
from jax import lax
from jax.sharding import Mesh
from jax.sharding import PartitionSpec as P

HEADS = 6
FEAT = ("feat_0", "feat_1")
GROUPS_FEAT = ("groups", "feat_0", "feat_1")


def split_up(x, dim, devices):
    before, after = (x.shape[:dim], x.shape[dim + 1 :])
    return jnp.moveaxis(x.reshape(*before, devices, -1, *after), dim, 0)


def joined_along(tiles, dim):
    tiles = jnp.moveaxis(tiles, 0, dim)
    lengths = tiles.shape
    return tiles.reshape(*lengths[:dim], lengths[dim] * lengths[dim + 1], *lengths[dim + 2 :])


def moved_by_axis(tiles, axes, sequence):
    inside = tiles.shape[1:]
    filled = tiles.reshape(*(lax.axis_size(a) for a in axes), *inside)
    for k in sequence:
        filled = lax.all_to_all(filled, axes[k], k, k, tiled=True)
    return filled.reshape(-1, *inside)


def core_and_chips(x, groups, sequence, split_dim, concat_dim):
    devices = lax.axis_size(groups[0]) * lax.axis_size(groups[1])
    tiles = split_up(x, split_dim, devices)
    return joined_along(moved_by_axis(tiles, groups, sequence), concat_dim)


def cell_norm(values, gain):
    mean = jnp.mean(values, axis=-1, keepdims=True)
    centered = values - mean
    var = jnp.mean(centered * centered, axis=-1, keepdims=True)
    return centered * lax.rsqrt(var + 1e-05) * gain


def attend(qkv):
    width = qkv.shape[-1] // 3
    count = qkv.shape[0]
    head_dim = width // HEADS
    query = qkv[:, :width].reshape(count, HEADS, head_dim)
    keys = qkv[:, width : 2 * width].reshape(count, HEADS, head_dim)
    values = qkv[:, 2 * width :].reshape(count, HEADS, head_dim)
    scores = jnp.einsum(
        "qhd,phd->hqp", query, keys, preferred_element_type=jnp.float32
    ) * head_dim ** (-0.5)
    top = jnp.max(scores, axis=-1, keepdims=True)
    expo = jnp.exp(scores - top)
    probs = (expo / jnp.sum(expo, axis=-1, keepdims=True)).astype(jnp.bfloat16)
    context = jnp.einsum("hqp,phd->qhd", probs, values, preferred_element_type=jnp.float32)
    return context.astype(jnp.bfloat16).reshape(count, width)


def finish(base, context, w_out, gain_two, w_up, w_down):
    mid = base + jnp.dot(context, w_out, preferred_element_type=jnp.float32)
    normed_two = cell_norm(mid, gain_two).astype(jnp.bfloat16)
    act = jax.nn.gelu(
        jnp.dot(normed_two, w_up, preferred_element_type=jnp.float32), approximate=False
    ).astype(jnp.bfloat16)
    return mid + jnp.dot(act, w_down, preferred_element_type=jnp.float32)


def body(
    cells, missing, feat_ids, feat_table, nan_embed, gain_one, w_qkv, w_out, gain_two, w_up, w_down
):
    devices = lax.axis_size(FEAT)
    all_rows, local_feats, width = cells.shape
    onehot = (
        feat_ids[:, None] == jnp.arange(feat_table.shape[0], dtype=jnp.int32)[None, :]
    ).astype(jnp.float32)
    femb = jnp.dot(onehot, feat_table, precision=lax.Precision.HIGHEST)
    tokens = (
        cells.astype(jnp.float32) + missing[..., None].astype(jnp.float32) * nan_embed + femb[None]
    ).astype(jnp.bfloat16)

    def one_row(row):
        base = row.astype(jnp.float32)
        normed = cell_norm(base, gain_one).astype(jnp.bfloat16)
        qkv = jnp.dot(normed, w_qkv, preferred_element_type=jnp.float32).astype(jnp.bfloat16)
        return finish(base, attend(qkv), w_out, gain_two, w_up, w_down)

    grouped = tokens.reshape(devices, all_rows // devices, local_feats, width)
    outputs = lax.map(one_row, core_and_chips(grouped, ("feat_0", "feat_1"), (1, 0), 0, 2)[0])
    back = core_and_chips(
        outputs[None].astype(jnp.bfloat16), ("feat_0", "feat_1"), (1, 0), 2, 0
    ).astype(jnp.float32)
    return back.reshape(all_rows, local_feats, width)


def solution(mesh):
    split = Mesh(mesh.devices.reshape(mesh.shape["groups"], 32, 2), ("groups", "feat_0", "feat_1"))
    in_specs = (
        P("groups", FEAT, None),
        P("groups", FEAT),
        P(GROUPS_FEAT),
        P(),
        P(),
        P(),
        P(),
        P(),
        P(),
        P(),
        P(),
    )
    out_specs = P("groups", FEAT, None)
    return jax.shard_map(body, mesh=split, in_specs=in_specs, out_specs=out_specs, check_vma=False)
```

profile of v0, /device:TPU:38, one launch (start us, length us, event | category | flops | bytes accessed | tf_op | source)
XLA Modules:
  0.0 265.7 jit_solution(11658586414275395537)
XLA Ops:
  0.0 0.7 convert_element_type.50
  0.9 0.8 fusion.102
  1.7 1.5 add_convert_fusion
  3.3 4.4 %all_to_all.20 = bf16[32,2,1,3,8,192]{5,4,3,0,2,1:T(8,128)(2,1)S(1)} all-to-all(bf16[32,2,1,3,8,192]{5,4,3,0,2,1:T(8,128)(2,1)S(1)} %copy.32), channel_id=1, replica_groups=mesh['groups'=4,'feat_0'=32,'feat_1'=2] {'feat_1'}, dimensions={1} | all-to-all | bytes 1179648 | tf_op jit(solution)/shard_map/all_to_all | solution.py:27
  7.6 0.9 copy.33
  8.6 32.7 %all-to-all-start.1 = ((bf16[32,2,1,3,8,192]{5,4,3,1,2,0:T(8,128)(2,1)}), bf16[32,2,1,3,8,192]{5,4,3,1,2,0:T(8,128)(2,1)S(1)}, u32[]{:S(2)}, u32[]{:S(2)}) async-start(bf16[32,2,1,3,8,192]{5,4,3,1,2,0:T(8,128)(2,1)} %copy.33), calls=%async_computation.1 | async-start | bytes 1572864 | tf_op jit(solution)/shard_map/all_to_all | solution.py:27
  41.3 86.6 %all-to-all-done.1 = bf16[32,2,1,3,8,192]{5,4,3,1,2,0:T(8,128)(2,1)S(1)} async-done(((bf16[32,2,1,3,8,192]{5,4,3,1,2,0:T(8,128)(2,1)}), bf16[32,2,1,3,8,192]{5,4,3,1,2,0:T(8,128)(2,1)S(1)}, u32[]{:S(2)}, u32[]{:S(2)}) %all-to-all-start.1) | async-done | bytes 589856 | tf_op jit(solution)/shard_map/all_to_all | solution.py:27
  128.3 39.8 %while.10 = (s32[]{:T(128)}, bf16[3,512,192]{1,2,0:T(8,128)(2,1)S(1)}, bf16[3,512,192]{1,2,0:T(8,128)(2,1)S(1)}, f32[192]{0:T(256)S(1)}, bf16[192,576]{1,0:T(8,1...) while((s32[]{:T(128)}, ...), condition=%wide.region_7.8_spmd, body=%wide.region_0.7_spmd.sunk | while | flops 690292224 | bytes 19060856 | solution.py:90
  128.5 0.4 convolution_convert_fusion.2
  129.0 4.8 %fusion.144 = (f32[6,512]{1,0:T(8,128)S(1)}, f32[6,512,512]{1,2,0:T(8,128)}) fusion(bf16[512,6,32]{0,2,1:T(8,128)(2,1)S(1)} %bitcast.85, bf16[512,6,32]{0,2,1:T(8,128)(2,1)S(1)} %bitcast.84), kind=kOutput, calls=%fused_computation.124.clone.1 | convolution fusion | flops 105382400 | bytes 6696960 | tf_op jit(solution)/shard_map/while/body/eval_jaxpr/sub | solution.py:55
  133.7 3.4 %fusion.145 = bf16[6,32,512]{2,1,0:T(8,128)(2,1)S(1)} fusion(bf16[512,6,32]{0,2,1:T(8,128)(2,1)S(1)} %bitcast.83, f32[6,512,512]{1,2,0:T(8,128)} %get-tuple-element.170, f32[6,512]{1,0:T(8,128)S(1)} %get-tuple-element.171), kind=kOutput, calls=%fused_computation.32.clone.1 | convolution fusion | flops 103907328 | bytes 6696960 | tf_op jit(solution)/shard_map/while/body/eval_jaxpr/hqp,phd->qhd/dot_general | solution.py:57
  137.2 0.3 fusion.146
  137.5 4.1 %fusion.147 = bf16[3,512,192]{1,2,0:T(8,128)(2,1)S(1)} fusion(bf16[3,512,192]{1,2,0:T(8,128)(2,1)S(1)} %get-tuple-element.185, s32[]{:T(128)} %get-tuple-element.184, f32[512,192]{0,1:T(8,128)S(1)} %get-tuple-element.172, bf16[768,192]{0,1:T(8,128)(2,1)S(1)} %get-tuple-element.202, bf16[192,768]{1,0:T(8,128)(2,1)S(1)} %get-tuple-element.201, ...), kind=kOutput, calls=%fused_computation.31.clone.1 | convolution fusion | flops 328040448 | bytes 1774596 | tf_op jit(solution)/shard_map/while/body/eval_jaxpr/dot_general | solution.py:67
  141.8 0.4 convolution_convert_fusion.2
  142.2 4.8 %fusion.144 = (f32[6,512]{1,0:T(8,128)S(1)}, f32[6,512,512]{1,2,0:T(8,128)}) fusion(bf16[512,6,32]{0,2,1:T(8,128)(2,1)S(1)} %bitcast.85, bf16[512,6,32]{0,2,1:T(8,128)(2,1)S(1)} %bitcast.84), kind=kOutput, calls=%fused_computation.124.clone.1 | convolution fusion | flops 105382400 | bytes 6696960 | tf_op jit(solution)/shard_map/while/body/eval_jaxpr/sub | solution.py:55
  147.0 3.4 %fusion.145 = bf16[6,32,512]{2,1,0:T(8,128)(2,1)S(1)} fusion(bf16[512,6,32]{0,2,1:T(8,128)(2,1)S(1)} %bitcast.83, f32[6,512,512]{1,2,0:T(8,128)} %get-tuple-element.170, f32[6,512]{1,0:T(8,128)S(1)} %get-tuple-element.171), kind=kOutput, calls=%fused_computation.32.clone.1 | convolution fusion | flops 103907328 | bytes 6696960 | tf_op jit(solution)/shard_map/while/body/eval_jaxpr/hqp,phd->qhd/dot_general | solution.py:57
  150.8 4.1 %fusion.147 = bf16[3,512,192]{1,2,0:T(8,128)(2,1)S(1)} fusion(bf16[3,512,192]{1,2,0:T(8,128)(2,1)S(1)} %get-tuple-element.185, s32[]{:T(128)} %get-tuple-element.184, f32[512,192]{0,1:T(8,128)S(1)} %get-tuple-element.172, bf16[768,192]{0,1:T(8,128)(2,1)S(1)} %get-tuple-element.202, bf16[192,768]{1,0:T(8,128)(2,1)S(1)} %get-tuple-element.201, ...), kind=kOutput, calls=%fused_computation.31.clone.1 | convolution fusion | flops 328040448 | bytes 1774596 | tf_op jit(solution)/shard_map/while/body/eval_jaxpr/dot_general | solution.py:67
  155.0 0.4 convolution_convert_fusion.2
  155.5 4.8 %fusion.144 = (f32[6,512]{1,0:T(8,128)S(1)}, f32[6,512,512]{1,2,0:T(8,128)}) fusion(bf16[512,6,32]{0,2,1:T(8,128)(2,1)S(1)} %bitcast.85, bf16[512,6,32]{0,2,1:T(8,128)(2,1)S(1)} %bitcast.84), kind=kOutput, calls=%fused_computation.124.clone.1 | convolution fusion | flops 105382400 | bytes 6696960 | tf_op jit(solution)/shard_map/while/body/eval_jaxpr/sub | solution.py:55
  160.3 3.4 %fusion.145 = bf16[6,32,512]{2,1,0:T(8,128)(2,1)S(1)} fusion(bf16[512,6,32]{0,2,1:T(8,128)(2,1)S(1)} %bitcast.83, f32[6,512,512]{1,2,0:T(8,128)} %get-tuple-element.170, f32[6,512]{1,0:T(8,128)S(1)} %get-tuple-element.171), kind=kOutput, calls=%fused_computation.32.clone.1 | convolution fusion | flops 103907328 | bytes 6696960 | tf_op jit(solution)/shard_map/while/body/eval_jaxpr/hqp,phd->qhd/dot_general | solution.py:57
  164.1 4.1 %fusion.147 = bf16[3,512,192]{1,2,0:T(8,128)(2,1)S(1)} fusion(bf16[3,512,192]{1,2,0:T(8,128)(2,1)S(1)} %get-tuple-element.185, s32[]{:T(128)} %get-tuple-element.184, f32[512,192]{0,1:T(8,128)S(1)} %get-tuple-element.172, bf16[768,192]{0,1:T(8,128)(2,1)S(1)} %get-tuple-element.202, bf16[192,768]{1,0:T(8,128)(2,1)S(1)} %get-tuple-element.201, ...), kind=kOutput, calls=%fused_computation.31.clone.1 | convolution fusion | flops 328040448 | bytes 1774596 | tf_op jit(solution)/shard_map/while/body/eval_jaxpr/dot_general | solution.py:67
  168.5 4.4 %all_to_all.21 = bf16[32,2,1,3,8,192]{5,4,0,3,2,1:T(8,128)(2,1)S(1)} all-to-all(bf16[32,2,1,3,8,192]{5,4,0,3,2,1:T(8,128)(2,1)S(1)} %copy.37), channel_id=1, replica_groups=mesh['groups'=4,'feat_0'=32,'feat_1'=2] {'feat_1'}, dimensions={1} | all-to-all | bytes 1179648 | tf_op jit(solution)/shard_map/all_to_all | solution.py:27
  172.9 91.4 %all_to_all.22 = bf16[32,2,1,3,8,192]{5,4,1,3,2,0:T(8,128)(2,1)S(1)} all-to-all(bf16[32,2,1,3,8,192]{5,4,1,3,2,0:T(8,128)(2,1)S(1)} %copy.38), channel_id=1, replica_groups=mesh['groups'=4,'feat_0'=32,'feat_1'=2] {'feat_0'}, dimensions={0} | all-to-all | bytes 1179648 | tf_op jit(solution)/shard_map/all_to_all | solution.py:27
  264.4 1.3 bitcast_convert_fusion
  (49 shorter events, 2.3 us)
Async XLA Ops:
  0.0 0.8 copy-start
  8.6 119.4 %all-to-all-start.1 = ((bf16[32,2,1,3,8,192]{5,4,3,1,2,0:T(8,128)(2,1)}), bf16[32,2,1,3,8,192]{5,4,3,1,2,0:T(8,128)(2,1)S(1)}, u32[]{:S(2)}, u32[]{:S(2)}) async-start(bf16[32,2,1,3,8,192]{5,4,3,1,2,0:T(8,128)(2,1)} %copy.33), calls=%async_computation.1 | async-start | bytes 1572864 | tf_op jit(solution)/shard_map/all_to_all | solution.py:27
  41.2 87.0 %copy-start.1 = (bf16[192,576]{1,0:T(8,128)(2,1)S(1)}, bf16[192,576]{1,0:T(8,128)(2,1)}, u32[]{:S(2)}) copy-start(bf16[192,576]{1,0:T(8,128)(2,1)} %param.19) | copy-start | bytes 663556
  41.3 87.0 %copy-start.2 = (bf16[192,192]{1,0:T(8,128)(2,1)S(1)}, bf16[192,192]{1,0:T(8,128)(2,1)}, u32[]{:S(2)}) copy-start(bf16[192,192]{1,0:T(8,128)(2,1)} %param.20) | copy-start | bytes 221188
  41.3 87.0 %copy-start.3 = (f32[192]{0:T(256)S(1)}, f32[192]{0:T(256)}, u32[]{:S(2)}) copy-start(f32[192]{0:T(256)} %param.18) | copy-start | bytes 2308
  41.3 87.0 %copy-start.4 = (bf16[192,768]{1,0:T(8,128)(2,1)S(1)}, bf16[192,768]{1,0:T(8,128)(2,1)}, u32[]{:S(2)}) copy-start(bf16[192,768]{1,0:T(8,128)(2,1)} %param.22) | copy-start | bytes 884740
  41.3 87.0 %copy-start.5 = (bf16[768,192]{0,1:T(8,128)(2,1)S(1)}, bf16[768,192]{0,1:T(8,128)(2,1)}, u32[]{:S(2)}) copy-start(bf16[768,192]{0,1:T(8,128)(2,1)} %param.23) | copy-start | bytes 884740
  41.3 87.0 %copy-start.6 = (f32[192]{0:T(256)S(1)}, f32[192]{0:T(256)}, u32[]{:S(2)}) copy-start(f32[192]{0:T(256)} %param.21) | copy-start | bytes 2308
where the time goes:
time: 266 us
  blocking collectives  100 us (38%)
  waiting for transfers between devices  86.6 us (33%)
  matrix products  39.7 us (15%)
  starting transfers between devices  32.7 us (12%)
  other arithmetic  4.23 us (2%)
    all_to_all x3, blocking collectives, moved_by_axis(): filled = lax.all_to_all(filled, axes[k], k, k, tiled=True)  100 us
    all_to_all x1, waiting for transfers between devices, moved_by_axis(): filled = lax.all_to_all(filled, axes[k], k, k, tiled=True)  86.6 us
    all_to_all x1, starting transfers between devices, moved_by_axis(): filled = lax.all_to_all(filled, axes[k], k, k, tiled=True)  32.7 us
    sub x3, matrix products, attend(): expo = jnp.exp(scores - top)  14.3 us
    dot_general x3, matrix products, finish(): return mid + jnp.dot(act, w_down, preferred_element_type=jnp.float32)  12.2 us
    dot_general x3, matrix products, attend(): jnp.einsum('hqp,phd->qhd', probs, values, preferred_element_type=jnp.floa...  10.3 us
  transfers between devices with their start and end apart: 1, of which 1 were waited for; matrix products, arithmetic and copies ran while one was open for 0% of the time, Pallas kernels for 0%

commit v1 on v0

v1 whole, which is shorter than its diff:
```python
import functools
import math

import jax
import jax.numpy as jnp
from jax import lax
from jax.experimental import pallas as pl
from jax.experimental.pallas import tpu as pltpu
from jax.sharding import Mesh
from jax.sharding import PartitionSpec as P

HEADS = 6
CORES = 2
LANES = 128
FEAT = ("chip", "core")
MESH = pl.DeviceIdType.MESH


def cell_norm(values, gain):
    mean = jnp.mean(values, axis=-1, keepdims=True)
    centered = values - mean
    var = jnp.mean(centered * centered, axis=-1, keepdims=True)
    return centered * lax.rsqrt(var + 1e-05) * gain


def gelu(x):
    return 0.5 * x * (1.0 + lax.erf(x * math.sqrt(0.5)))


def kernel(
    n,
    phases,
    cells_ref,
    missing_ref,
    ids_ref,
    table_ref,
    nan_ref,
    gain_one_ref,
    w_qkv_ref,
    w_out_ref,
    gain_two_ref,
    w_up_ref,
    w_down_ref,
    out_ref,
    x_ref,
    rx_ref,
    tx_ref,
    y_ref,
    w_ref,
    q_ref,
    k_ref,
    v_ref,
    ctx_ref,
    f_send,
    f_recv,
    kv_send,
    kv_recv,
    b_send,
    b_recv,
):
    me = lax.axis_index("chip")
    core = lax.axis_index("core")
    rows, feats, width = cells_ref.shape
    per_chip = rows // n
    half = n * feats
    rest = width - LANES
    head_dim = width // HEADS

    def chip_at(k):
        return lax.rem(me + k, n)

    barrier = pltpu.get_barrier_semaphore()
    pl.semaphore_signal(barrier, inc=1, device_id={"core": 1 - core}, device_id_type=MESH)
    for k in range(1, n):
        pl.semaphore_signal(barrier, inc=1, device_id={"chip": chip_at(k)}, device_id_type=MESH)

    for i in range(3):
        w_ref[i] = w_qkv_ref[:, i * width : (i + 1) * width]

    spot = lax.broadcasted_iota(jnp.int32, (table_ref.shape[0], feats), 0)
    onehot = (spot == ids_ref[...]).astype(jnp.float32)
    femb = lax.dot_general(
        onehot,
        table_ref[...],
        (((0,), (0,)), ((), ())),
        precision=lax.Precision.HIGHEST,
        preferred_element_type=jnp.float32,
    )
    chips_step = 8 if n % 8 == 0 else n
    step = per_chip * chips_step
    cells_step = step * feats

    def make_tokens(i, carry):
        start = pl.multiple_of(i * step, 8)
        miss = missing_ref[pl.ds(start, step), :].astype(jnp.float32).astype(jnp.bfloat16)
        line = lax.broadcasted_iota(jnp.int32, (cells_step, step), 0)
        column = lax.broadcasted_iota(jnp.int32, (cells_step, step), 1)
        pick = jnp.where(line // feats == column, 1.0, 0.0).astype(jnp.bfloat16)
        spread = jnp.dot(pick, miss, preferred_element_type=jnp.float32)
        line = lax.broadcasted_iota(jnp.int32, (cells_step, feats), 0)
        column = lax.broadcasted_iota(jnp.int32, (cells_step, feats), 1)
        flag = jnp.sum(jnp.where(line % feats == column, spread, 0.0), axis=-1, keepdims=True)
        tokens = (
            cells_ref[pl.ds(start, step)].astype(jnp.float32)
            + (flag * nan_ref[...]).reshape(step, feats, width)
            + femb[None]
        )
        head = tokens[:, :, :LANES].astype(jnp.bfloat16).reshape(chips_step, phases, 2, feats, LANES)
        tail = tokens[:, :, LANES:].reshape(chips_step * phases, 2, feats, rest)
        tail = jnp.concatenate([tail[:, 0], tail[:, 1]], axis=-1).astype(jnp.bfloat16)
        tail = tail.reshape(chips_step, phases, feats, LANES)
        chips = pl.ds(i * chips_step, chips_step)
        for p in range(phases):
            x_ref[p, chips, :feats, :] = head[:, p, 0]
            x_ref[p, chips, feats : 2 * feats, :] = head[:, p, 1]
            x_ref[p, chips, 2 * feats :, :] = tail[:, p]
        return carry

    lax.fori_loop(0, rows // step, make_tokens, 0)
    pl.semaphore_wait(barrier, n)

    def forward(p, k):
        return pltpu.make_async_remote_copy(
            src_ref=x_ref.at[p, chip_at(k)],
            dst_ref=rx_ref.at[p, k],
            send_sem=f_send.at[p],
            recv_sem=f_recv.at[p],
            device_id={"chip": chip_at(k)},
            device_id_type=MESH,
        )

    def backward(p, k):
        return pltpu.make_async_remote_copy(
            src_ref=tx_ref.at[p, k],
            dst_ref=y_ref.at[p, k],
            send_sem=b_send.at[p],
            recv_sem=b_recv.at[p],
            device_id={"chip": chip_at(n - k)},
            device_id_type=MESH,
        )

    def send_all(copy, p):
        copy(p, n // 2).start()

        def pair(i, carry):
            far = n // 2 - 1 - i
            copy(p, far).start()
            copy(p, n - far).start()
            return carry

        lax.fori_loop(0, n // 2 - 1, pair, 0)

    def whole(src, dst, send, recv, p):
        return pltpu.make_async_remote_copy(
            src_ref=src.at[p, pl.ds(1, n - 1)],
            dst_ref=dst.at[p, pl.ds(1, n - 1)],
            send_sem=send.at[p],
            recv_sem=recv.at[p],
            device_id={"chip": chip_at(1)},
            device_id_type=MESH,
        )

    def swap(p, which):
        ref = (k_ref, v_ref)[which]
        return pltpu.make_async_remote_copy(
            src_ref=ref.at[p, :, pl.ds(0, half)],
            dst_ref=ref.at[p, :, pl.ds(half, half)],
            send_sem=kv_send.at[p, which],
            recv_sem=kv_recv.at[p, which],
            device_id={"core": 1 - core},
            device_id_type=MESH,
        )

    lax.fori_loop(0, phases, lambda p, c: (send_all(forward, p), c)[1], 0)

    def base_of(p, r):
        first = rx_ref[p, :, r * feats : (r + 1) * feats, :].astype(jnp.float32).reshape(half, LANES)
        last = rx_ref[p, :, 2 * feats :, :].astype(jnp.float32).reshape(half, LANES)
        return jnp.concatenate([first, last[:, r * rest : (r + 1) * rest]], axis=-1)

    def phase(p, carry):
        rx_ref[p, 0] = x_ref[p, me]
        whole(x_ref, rx_ref, f_send, f_recv, p).wait_recv()
        for r in range(2):
            normed = cell_norm(base_of(p, r), gain_one_ref[...]).astype(jnp.bfloat16)
            for ref, i in ((k_ref, 1), (v_ref, 2)):
                made = jnp.dot(normed, w_ref[i], preferred_element_type=jnp.float32)
                ref[p, r, :half] = made.astype(jnp.bfloat16)
            made = jnp.dot(normed, w_ref[0], preferred_element_type=jnp.float32)
            q_ref[r] = made.astype(jnp.bfloat16)
        for which in range(2):
            swap(p, which).start()
        for which in range(2):
            swap(p, which).wait_recv()

        lane_head = lax.broadcasted_iota(jnp.int32, (half, width), 1) // head_dim
        results = []
        for r in range(2):

            def one_head(h, carry):
                mine = lane_head == h
                query = jnp.where(mine, q_ref[r].astype(jnp.float32), 0.0).astype(jnp.bfloat16)
                scores = lax.dot_general(
                    query, k_ref[p, r], (((1,), (1,)), ((), ())), preferred_element_type=jnp.float32
                )
                top = jnp.max(scores, axis=-1, keepdims=True)
                expo = jnp.exp2((scores - top) * (head_dim**-0.5 * math.log2(math.e)))
                probs = expo * (1.0 / jnp.sum(expo, axis=-1, keepdims=True))
                got = jnp.dot(
                    probs.astype(jnp.bfloat16), v_ref[p, r], preferred_element_type=jnp.float32
                )
                ctx_ref[...] = jnp.where(mine, got.astype(jnp.bfloat16), ctx_ref[...])
                return carry

            lax.fori_loop(0, HEADS, one_head, 0)
            mid = base_of(p, r) + jnp.dot(
                ctx_ref[...], w_out_ref[...], preferred_element_type=jnp.float32
            )
            normed = cell_norm(mid, gain_two_ref[...]).astype(jnp.bfloat16)
            act = gelu(jnp.dot(normed, w_up_ref[...], preferred_element_type=jnp.float32))
            result = mid + jnp.dot(
                act.astype(jnp.bfloat16), w_down_ref[...], preferred_element_type=jnp.float32
            )
            tx_ref[p, :, r * feats : (r + 1) * feats, :] = (
                result[:, :LANES].astype(jnp.bfloat16).reshape(n, feats, LANES)
            )
            results.append(result[:, LANES:])
        tail = jnp.concatenate(results, axis=-1).astype(jnp.bfloat16)
        tx_ref[p, :, 2 * feats :, :] = tail.reshape(n, feats, LANES)
        send_all(backward, p)
        y_ref[p, 0] = tx_ref[p, 0]
        return carry

    lax.fori_loop(0, phases, phase, 0)

    def place(p, carry):
        whole(tx_ref, y_ref, b_send, b_recv, p).wait_recv()

        def one(k, carry):
            row = chip_at(k) * per_chip + 2 * p
            last = y_ref[p, k, 2 * feats :, :]
            for r in range(2):
                first = y_ref[p, k, r * feats : (r + 1) * feats, :]
                out_ref[row + r] = jnp.concatenate(
                    [first, last[:, r * rest : (r + 1) * rest]], axis=-1
                )
            return carry

        lax.fori_loop(0, n, one, 0)
        return carry

    lax.fori_loop(0, phases, place, 0)

    def drain(p, carry):
        whole(x_ref, rx_ref, f_send, f_recv, p).wait_send()
        whole(tx_ref, y_ref, b_send, b_recv, p).wait_send()
        for which in range(2):
            swap(p, which).wait_send()
        return carry

    lax.fori_loop(0, phases, drain, 0)


def solution(mesh):
    groups = mesh.shape["groups"]
    n = mesh.shape["feat"] // CORES
    split = Mesh(mesh.devices.reshape(groups, n, CORES), ("groups", *FEAT))

    def body(
        cells, missing, feat_ids, table, nan_embed, gain_one, w_qkv, w_out, gain_two, w_up, w_down
    ):
        rows, feats, width = cells.shape
        phases = rows // n // 2
        packed = pltpu.VMEM((phases, n, 3 * feats, LANES), jnp.bfloat16)
        half = n * feats
        keys = pltpu.VMEM((phases, 2, CORES * half, width), jnp.bfloat16)
        dma = pltpu.SemaphoreType.DMA
        out = pl.pallas_call(
            functools.partial(kernel, n, phases),
            out_shape=jax.ShapeDtypeStruct(cells.shape, jnp.bfloat16),
            in_specs=[pl.BlockSpec(memory_space=pltpu.VMEM)] * 11,
            out_specs=pl.BlockSpec(memory_space=pltpu.VMEM),
            scratch_shapes=[
                packed,
                packed,
                packed,
                packed,
                pltpu.VMEM((3, width, width), jnp.bfloat16),
                pltpu.VMEM((2, half, width), jnp.bfloat16),
                keys,
                keys,
                pltpu.VMEM((half, width), jnp.bfloat16),
                dma((phases,)),
                dma((phases,)),
                dma((phases, 2)),
                dma((phases, 2)),
                dma((phases,)),
                dma((phases,)),
            ],
            compiler_params=pltpu.CompilerParams(collective_id=0, has_side_effects=True),
        )(
            cells,
            missing,
            feat_ids[None],
            table,
            nan_embed[None],
            gain_one[None],
            w_qkv,
            w_out,
            gain_two[None],
            w_up,
            w_down,
        )
        return out.astype(jnp.float32)

    spread = P("groups", FEAT, None)
    in_specs = (spread, P("groups", FEAT), P(("groups", *FEAT))) + (P(),) * 8
    return jax.shard_map(
        body, mesh=split, in_specs=in_specs, out_specs=spread, check_vma=False
    )
```

time: 266 us -> 146 us (0.55)
  the two profiles are of different devices: /device:TPU:38 before, /device:TPU:44 now
where the time goes in v1:
time: 146 us
  Pallas kernels  140 us (96%)
  local copies, waits for them, and re-layouts  3.32 us (2%)
  other arithmetic  2.39 us (2%)
    pallas_call x1, Pallas kernels, body(): pl.pallas_call(functools.partial(kernel, n, phases), out_shape=jax.ShapeD...  140 us
    unnamed x2, local copies, waits for them, and re-layouts  3.32 us

profile of v1, /device:TPU:44, one launch (start us, length us, event | category | flops | bytes accessed | tf_op | source)
XLA Modules:
  0.0 145.8 jit_solution(13506797730064687900)
XLA Ops:
  0.0 1.4 copy.12.missing_ref
  1.4 1.9 %copy.13.w_down_ref = bf16[768,192]{1,0:T(8,128)(2,1)} copy(bf16[768,192]{0,1:T(8,128)(2,1)} %param.21) | data formatting | bytes 589824 | tf_op args[10]
  3.3 140.1 %shard_map.109 = bf16[192,8,192]{2,1,0:T(8,128)(2,1)} custom-call(bf16[192,8,192]{2,1,0:T(8,128)(2,1)} %cells_ref.1, s32[192,8]{1,0:T(8,128)} %copy.12.missing_ref, s32[1,8]{1,0:T(1,128)} %bitcast.7, f32[64,192]{1,0:T(8,128)} %table_ref.1, f32[1,192]{1,0:T(1,128)} %bitcast.4, f32[1,192]{1,0:T(1,128)} %bitcast.5, bf16[192,576]{1,0:T(8,128)(2,1)} %w_qkv_ref.1, ...), custom_call_target="tpu_custom_call" | custom-call | tf_op jit(solution)/shard_map/pallas_call | solution.py:278
  143.4 2.4 %convert_element_type.3 = f32[192,8,192]{2,1,0:T(8,128)} convert(bf16[192,8,192]{2,1,0:T(8,128)(2,1)} %shard_map.109) | non-fusion elementwise | flops 294912 | bytes 1769472 | tf_op jit(solution)/shard_map/convert_element_type | solution.py:314

commit v2 on v1

--- a/solution.py
+++ b/solution.py
@@ -30,6 +30,18 @@
 def kernel(
     n,
     phases,
+    cells_hbm,
+    missing_hbm,
+    ids_hbm,
+    table_hbm,
+    nan_hbm,
+    gain_one_hbm,
+    w_qkv_hbm,
+    w_out_hbm,
+    gain_two_hbm,
+    w_up_hbm,
+    w_down_hbm,
+    y_ref,
     cells_ref,
     missing_ref,
     ids_ref,
@@ -41,16 +53,17 @@
     gain_two_ref,
     w_up_ref,
     w_down_ref,
-    out_ref,
     x_ref,
     rx_ref,
     tx_ref,
-    y_ref,
     w_ref,
     q_ref,
     k_ref,
     v_ref,
     ctx_ref,
+    c_sem,
+    in_sem,
+    own_sem,
     f_send,
     f_recv,
     kv_send,
@@ -60,8 +73,9 @@
 ):
     me = lax.axis_index("chip")
     core = lax.axis_index("core")
-    rows, feats, width = cells_ref.shape
-    per_chip = rows // n
+    feats, width = cells_ref.shape[3:]
+    per_chip = 2 * phases
+    rows = n * per_chip
     half = n * feats
     rest = width - LANES
     head_dim = width // HEADS
@@ -74,8 +88,31 @@
     for k in range(1, n):
         pl.semaphore_signal(barrier, inc=1, device_id={"chip": chip_at(k)}, device_id_type=MESH)
 
-    for i in range(3):
-        w_ref[i] = w_qkv_ref[:, i * width : (i + 1) * width]
+    first = [
+        (missing_hbm, missing_ref),
+        (ids_hbm, ids_ref),
+        (table_hbm, table_ref),
+        (nan_hbm, nan_ref),
+    ]
+    later = [
+        (gain_one_hbm, gain_one_ref),
+        (w_qkv_hbm, w_qkv_ref),
+        (w_out_hbm, w_out_ref),
+        (gain_two_hbm, gain_two_ref),
+        (w_up_hbm, w_up_ref),
+        (w_down_hbm, w_down_ref),
+    ]
+    loads = [
+        pltpu.make_async_copy(src, dst, in_sem.at[i]) for i, (src, dst) in enumerate(first + later)
+    ]
+    cell_loads = [
+        pltpu.make_async_copy(cells_hbm.at[:, p], cells_ref.at[p], c_sem.at[p])
+        for p in range(phases)
+    ]
+    for load in loads[: len(first)] + cell_loads + loads[len(first) :]:
+        load.start()
+    for load in loads[: len(first)]:
+        load.wait()
 
     spot = lax.broadcasted_iota(jnp.int32, (table_ref.shape[0], feats), 0)
     onehot = (spot == ids_ref[...]).astype(jnp.float32)
@@ -86,38 +123,30 @@
         precision=lax.Precision.HIGHEST,
         preferred_element_type=jnp.float32,
     )
-    chips_step = 8 if n % 8 == 0 else n
-    step = per_chip * chips_step
-    cells_step = step * feats
-
-    def make_tokens(i, carry):
-        start = pl.multiple_of(i * step, 8)
-        miss = missing_ref[pl.ds(start, step), :].astype(jnp.float32).astype(jnp.bfloat16)
-        line = lax.broadcasted_iota(jnp.int32, (cells_step, step), 0)
-        column = lax.broadcasted_iota(jnp.int32, (cells_step, step), 1)
-        pick = jnp.where(line // feats == column, 1.0, 0.0).astype(jnp.bfloat16)
-        spread = jnp.dot(pick, miss, preferred_element_type=jnp.float32)
-        line = lax.broadcasted_iota(jnp.int32, (cells_step, feats), 0)
-        column = lax.broadcasted_iota(jnp.int32, (cells_step, feats), 1)
+    miss = missing_ref[...].astype(jnp.float32).astype(jnp.bfloat16)
+    count = n * 2 * feats
+
+    def make_tokens(p):
+        line = lax.broadcasted_iota(jnp.int32, (count, rows), 0) // feats
+        column = lax.broadcasted_iota(jnp.int32, (count, rows), 1)
+        row = (line // 2) * per_chip + 2 * p + line % 2
+        pick = jnp.where(row == column, 1.0, 0.0).astype(jnp.bfloat16)
+        spread = lax.dot_general(
+            pick, miss, (((1,), (1,)), ((), ())), preferred_element_type=jnp.float32
+        )
+        line = lax.broadcasted_iota(jnp.int32, (count, feats), 0)
+        column = lax.broadcasted_iota(jnp.int32, (count, feats), 1)
         flag = jnp.sum(jnp.where(line % feats == column, spread, 0.0), axis=-1, keepdims=True)
+        cell_loads[p].wait()
         tokens = (
-            cells_ref[pl.ds(start, step)].astype(jnp.float32)
-            + (flag * nan_ref[...]).reshape(step, feats, width)
-            + femb[None]
-        )
-        head = tokens[:, :, :LANES].astype(jnp.bfloat16).reshape(chips_step, phases, 2, feats, LANES)
-        tail = tokens[:, :, LANES:].reshape(chips_step * phases, 2, feats, rest)
-        tail = jnp.concatenate([tail[:, 0], tail[:, 1]], axis=-1).astype(jnp.bfloat16)
-        tail = tail.reshape(chips_step, phases, feats, LANES)
-        chips = pl.ds(i * chips_step, chips_step)
-        for p in range(phases):
-            x_ref[p, chips, :feats, :] = head[:, p, 0]
-            x_ref[p, chips, feats : 2 * feats, :] = head[:, p, 1]
-            x_ref[p, chips, 2 * feats :, :] = tail[:, p]
-        return carry
-
-    lax.fori_loop(0, rows // step, make_tokens, 0)
-    pl.semaphore_wait(barrier, n)
+            cells_ref[p].astype(jnp.float32)
+            + (flag * nan_ref[...]).reshape(n, 2, feats, width)
+            + femb[None, None]
+        )
+        for r in range(2):
+            x_ref[p, :, r * feats : (r + 1) * feats, :] = tokens[:, r, :, :LANES].astype(jnp.bfloat16)
+        tail = jnp.concatenate([tokens[:, 0, :, LANES:], tokens[:, 1, :, LANES:]], axis=-1)
+        x_ref[p, :, 2 * feats :, :] = tail.astype(jnp.bfloat16)
 
     def forward(p, k):
         return pltpu.make_async_remote_copy(
@@ -132,7 +161,7 @@
     def backward(p, k):
         return pltpu.make_async_remote_copy(
             src_ref=tx_ref.at[p, k],
-            dst_ref=y_ref.at[p, k],
+            dst_ref=y_ref.at[p, me],
             send_sem=b_send.at[p],
             recv_sem=b_recv.at[p],
             device_id={"chip": chip_at(n - k)},
@@ -171,7 +200,19 @@
             device_id_type=MESH,
         )
 
-    lax.fori_loop(0, phases, lambda p, c: (send_all(forward, p), c)[1], 0)
+    for p in range(phases):
+        make_tokens(p)
+        if p == 0:
+            pl.semaphore_wait(barrier, n)
+        send_all(forward, p)
+
+    for load in loads[len(first) :]:
+        load.wait()
+    for i in range(3):
+        w_ref[i] = w_qkv_ref[:, i * width : (i + 1) * width]
+
+    def own(p):
+        return pltpu.make_async_copy(tx_ref.at[p, 0], y_ref.at[p, me], own_sem.at[p])
 
     def base_of(p, r):
         first = rx_ref[p, :, r * feats : (r + 1) * feats, :].astype(jnp.float32).reshape(half, LANES)
@@ -218,8 +259,11 @@
             )
             normed = cell_norm(mid, gain_two_ref[...]).astype(jnp.bfloat16)
             act = gelu(jnp.dot(normed, w_up_ref[...], preferred_element_type=jnp.float32))
-            result = mid + jnp.dot(
-                act.astype(jnp.bfloat16), w_down_ref[...], preferred_element_type=jnp.float32
+            result = mid + lax.dot_general(
+                act.astype(jnp.bfloat16),
+                w_down_ref[...],
+                (((1,), (1,)), ((), ())),
+                preferred_element_type=jnp.float32,
             )
             tx_ref[p, :, r * feats : (r + 1) * feats, :] = (
                 result[:, :LANES].astype(jnp.bfloat16).reshape(n, feats, LANES)
@@ -228,30 +272,14 @@
         tail = jnp.concatenate(results, axis=-1).astype(jnp.bfloat16)
         tx_ref[p, :, 2 * feats :, :] = tail.reshape(n, feats, LANES)
         send_all(backward, p)
-        y_ref[p, 0] = tx_ref[p, 0]
+        own(p).start()
         return carry
 
     lax.fori_loop(0, phases, phase, 0)
 
-    def place(p, carry):
+    def drain(p, carry):
         whole(tx_ref, y_ref, b_send, b_recv, p).wait_recv()
-
-        def one(k, carry):
-            row = chip_at(k) * per_chip + 2 * p
-            last = y_ref[p, k, 2 * feats :, :]
-            for r in range(2):
-                first = y_ref[p, k, r * feats : (r + 1) * feats, :]
-                out_ref[row + r] = jnp.concatenate(
-                    [first, last[:, r * rest : (r + 1) * rest]], axis=-1
-                )
-            return carry
-
-        lax.fori_loop(0, n, one, 0)
-        return carry
-
-    lax.fori_loop(0, phases, place, 0)
-
-    def drain(p, carry):
+        own(p).wait()
         whole(x_ref, rx_ref, f_send, f_recv, p).wait_send()
         whole(tx_ref, y_ref, b_send, b_recv, p).wait_send()
         for which in range(2):
@@ -259,6 +287,18 @@
         return carry
 
     lax.fori_loop(0, phases, drain, 0)
+
+
+def unpack(y_ref, out_ref):
+    phases = out_ref.shape[1]
+    feats, width = out_ref.shape[3:]
+    rest = width - LANES
+    for p in range(phases):
+        last = y_ref[p, :, 2 * feats :, :].astype(jnp.float32)
+        for r in range(2):
+            first = y_ref[p, :, r * feats : (r + 1) * feats, :].astype(jnp.float32)
+            out_ref[:, p, r, :, :LANES] = first
+            out_ref[:, p, r, :, LANES:] = last[:, :, r * rest : (r + 1) * rest]
 
 
 def solution(mesh):
@@ -275,21 +315,36 @@
         half = n * feats
         keys = pltpu.VMEM((phases, 2, CORES * half, width), jnp.bfloat16)
         dma = pltpu.SemaphoreType.DMA
-        out = pl.pallas_call(
+        vmem = pltpu.VMEM
+        anywhere = pl.BlockSpec(memory_space=pl.ANY)
+        y = pl.pallas_call(
             functools.partial(kernel, n, phases),
-            out_shape=jax.ShapeDtypeStruct(cells.shape, jnp.bfloat16),
-            in_specs=[pl.BlockSpec(memory_space=pltpu.VMEM)] * 11,
-            out_specs=pl.BlockSpec(memory_space=pltpu.VMEM),
+            out_shape=jax.ShapeDtypeStruct(packed.shape, jnp.bfloat16),
+            in_specs=[anywhere] * 11,
+            out_specs=anywhere,
             scratch_shapes=[
+                vmem((phases, n, 2, feats, width), cells.dtype),
+                vmem((feats, rows), missing.dtype),
+                vmem((1, feats), feat_ids.dtype),
+                vmem(table.shape, table.dtype),
+                vmem((1, width), nan_embed.dtype),
+                vmem((1, width), gain_one.dtype),
+                vmem(w_qkv.shape, w_qkv.dtype),
+                vmem(w_out.shape, w_out.dtype),
+                vmem((1, width), gain_two.dtype),
+                vmem(w_up.shape, w_up.dtype),
+                vmem(w_down.shape[::-1], w_down.dtype),
                 packed,
                 packed,
                 packed,
-                packed,
-                pltpu.VMEM((3, width, width), jnp.bfloat16),
-                pltpu.VMEM((2, half, width), jnp.bfloat16),
+                vmem((3, width, width), jnp.bfloat16),
+                vmem((2, half, width), jnp.bfloat16),
                 keys,
                 keys,
-                pltpu.VMEM((half, width), jnp.bfloat16),
+                vmem((half, width), jnp.bfloat16),
+                dma((phases,)),
+                dma((10,)),
+                dma((phases,)),
                 dma((phases,)),
                 dma((phases,)),
                 dma((phases, 2)),
@@ -299,8 +354,8 @@
             ],
             compiler_params=pltpu.CompilerParams(collective_id=0, has_side_effects=True),
         )(
-            cells,
-            missing,
+            cells.reshape(n, phases, 2, feats, width),
+            missing.T,
             feat_ids[None],
             table,
             nan_embed[None],
@@ -309,9 +364,17 @@
             w_out,
             gain_two[None],
             w_up,
-            w_down,
-        )
-        return out.astype(jnp.float32)
+            w_down.T,
+        )
+        steps = 4 if n % 4 == 0 else 1
+        out = pl.pallas_call(
+            unpack,
+            grid=(steps,),
+            out_shape=jax.ShapeDtypeStruct((n, phases, 2, feats, width), jnp.float32),
+            in_specs=[pl.BlockSpec((phases, n // steps, 3 * feats, LANES), lambda i: (0, i, 0, 0))],
+            out_specs=pl.BlockSpec((n // steps, phases, 2, feats, width), lambda i: (i, 0, 0, 0, 0)),
+        )(y)
+        return out.reshape(rows, feats, width)
 
     spread = P("groups", FEAT, None)
     in_specs = (spread, P("groups", FEAT), P(("groups", *FEAT))) + (P(),) * 8

time: 146 us -> 140 us (0.959)
  the two profiles are of different devices: /device:TPU:44 before, /device:TPU:38 now
where the time goes in v2:
time: 140 us; the launch traced here: 139 us
  Pallas kernels  139 us (99%)
    pallas_call x1, Pallas kernels, body(): pl.pallas_call(functools.partial(kernel, n, phases), out_shape=jax.ShapeD...  136 us
    pallas_call x1, Pallas kernels, body(): pl.pallas_call(unpack, grid=(steps,), out_shape=jax.ShapeDtypeStruct((n,...  3.52 us

profile of v2, /device:TPU:38, one launch (start us, length us, event | category | flops | bytes accessed | tf_op | source)
XLA Modules:
  0.0 139.3 jit_solution(14425891412445667080)
XLA Ops:
  0.0 135.8 %shard_map.109.y_ref = bf16[3,32,24,128]{3,2,1,0:T(8,128)(2,1)} custom-call(bf16[32,3,2,8,192]{4,3,2,1,0:T(8,128)(2,1)} %bitcast.8, s32[8,192]{1,0:T(8,128)} %bitcast.10, s32[1,8]{1,0:T(1,128)} %bitcast.14, f32[64,192]{1,0:T(8,128)} %table_hbm.1, f32[1,192]{1,0:T(1,128)} %bitcast.11, f32[1,192]{1,0:T(1,128)} %bitcast.12, bf16[192,576]{1,0:T(8,128)(2,1)} %w_qkv_hbm.1, ...), custom_call_target="tpu_custom_call" | custom-call | tf_op jit(solution)/shard_map/pallas_call | solution.py:320
  135.8 3.5 %shard_map.110 = f32[32,3,2,8,192]{4,3,2,1,0:T(8,128)} custom-call(bf16[3,32,24,128]{3,2,1,0:T(8,128)(2,1)} %shard_map.109.y_ref), custom_call_target="tpu_custom_call" | custom-call | tf_op jit(solution)/shard_map/pallas_call | solution.py:370

commit v3 on v2

--- a/solution.py
+++ b/solution.py
@@ -179,6 +179,17 @@
 
         lax.fori_loop(0, n // 2 - 1, pair, 0)
 
+    def send_to(low, high, *which):
+        def one(t, carry):
+            @pl.when(t != me)
+            def _():
+                for p in which:
+                    backward(p, lax.rem(me + n - t, n)).start()
+
+            return carry
+
+        lax.fori_loop(low, high, one, 0)
+
     def whole(src, dst, send, recv, p):
         return pltpu.make_async_remote_copy(
             src_ref=src.at[p, pl.ds(1, n - 1)],
@@ -271,11 +282,16 @@
             results.append(result[:, LANES:])
         tail = jnp.concatenate(results, axis=-1).astype(jnp.bfloat16)
         tx_ref[p, :, 2 * feats :, :] = tail.reshape(n, feats, LANES)
-        send_all(backward, p)
+
+        @pl.when(p == 0)
+        def _():
+            send_to(0, n, p)
+
         own(p).start()
         return carry
 
     lax.fori_loop(0, phases, phase, 0)
+    send_to(0, n, 1, 2)
 
     def drain(p, carry):
         whole(tx_ref, y_ref, b_send, b_recv, p).wait_recv()

time: 140 us -> 134 us (0.957)
  the two profiles are of different devices: /device:TPU:38 before, /device:TPU:431 now
where the time goes in v3:
time: 134 us
  Pallas kernels  134 us (100%)
    pallas_call x1, Pallas kernels, body(): pl.pallas_call(functools.partial(kernel, n, phases), out_shape=jax.ShapeD...  130 us
    pallas_call x1, Pallas kernels, body(): pl.pallas_call(unpack, grid=(steps,), out_shape=jax.ShapeDtypeStruct((n,...  3.52 us

profile of v3, /device:TPU:431, one launch (start us, length us, event | category | flops | bytes accessed | tf_op | source)
XLA Modules:
  0.0 133.7 jit_solution(2662479438901710988)
XLA Ops:
  0.0 130.1 %shard_map.109.y_ref = bf16[3,32,24,128]{3,2,1,0:T(8,128)(2,1)} custom-call(bf16[32,3,2,8,192]{4,3,2,1,0:T(8,128)(2,1)} %bitcast.8, s32[8,192]{1,0:T(8,128)} %bitcast.10, s32[1,8]{1,0:T(1,128)} %bitcast.14, f32[64,192]{1,0:T(8,128)} %table_hbm.1, f32[1,192]{1,0:T(1,128)} %bitcast.11, f32[1,192]{1,0:T(1,128)} %bitcast.12, bf16[192,576]{1,0:T(8,128)(2,1)} %w_qkv_hbm.1, ...), custom_call_target="tpu_custom_call" | custom-call | tf_op jit(solution)/shard_map/pallas_call | solution.py:336
  130.1 3.5 %shard_map.110 = f32[32,3,2,8,192]{4,3,2,1,0:T(8,128)} custom-call(bf16[3,32,24,128]{3,2,1,0:T(8,128)(2,1)} %shard_map.109.y_ref), custom_call_target="tpu_custom_call" | custom-call | tf_op jit(solution)/shard_map/pallas_call | solution.py:386

commit v4 on v3

--- a/solution.py
+++ b/solution.py
@@ -64,6 +64,7 @@
     c_sem,
     in_sem,
     own_sem,
+    heard,
     f_send,
     f_recv,
     kv_send,
@@ -83,10 +84,25 @@
     def chip_at(k):
         return lax.rem(me + k, n)
 
+    near = n // 4
     barrier = pltpu.get_barrier_semaphore()
     pl.semaphore_signal(barrier, inc=1, device_id={"core": 1 - core}, device_id_type=MESH)
     for k in range(1, n):
-        pl.semaphore_signal(barrier, inc=1, device_id={"chip": chip_at(k)}, device_id_type=MESH)
+        ear = 0 if min(k, n - k) <= near else 1
+        pl.semaphore_signal(
+            barrier, inc=1, device_id={"chip": chip_at(k), "core": ear}, device_id_type=MESH
+        )
+
+    def meet(which, count):
+        @pl.when(core == which)
+        def _():
+            pl.semaphore_wait(barrier, CORES * count + 1)
+            pl.semaphore_signal(heard, inc=1, device_id={"core": 1 - core}, device_id_type=MESH)
+
+    def hear(which):
+        @pl.when(core != which)
+        def _():
+            pl.semaphore_wait(heard, 1)
 
     first = [
         (missing_hbm, missing_ref),
@@ -168,16 +184,13 @@
             device_id_type=MESH,
         )
 
-    def send_all(copy, p):
-        copy(p, n // 2).start()
-
+    def send_pairs(copy, p, low, high):
         def pair(i, carry):
-            far = n // 2 - 1 - i
-            copy(p, far).start()
-            copy(p, n - far).start()
+            copy(p, high - i).start()
+            copy(p, n - high + i).start()
             return carry
 
-        lax.fori_loop(0, n // 2 - 1, pair, 0)
+        lax.fori_loop(0, high - low + 1, pair, 0)
 
     def send_to(low, high, *which):
         def one(t, carry):
@@ -211,11 +224,18 @@
             device_id_type=MESH,
         )
 
+    make_tokens(0)
+    meet(0, 2 * near)
+    hear(0)
     for p in range(phases):
-        make_tokens(p)
-        if p == 0:
-            pl.semaphore_wait(barrier, n)
-        send_all(forward, p)
+        if p > 0:
+            make_tokens(p)
+        send_pairs(forward, p, 1, near)
+    meet(1, n - 1 - 2 * near)
+    hear(1)
+    for p in range(phases):
+        forward(p, n // 2).start()
+        send_pairs(forward, p, near + 1, n // 2 - 1)
 
     for load in loads[len(first) :]:
         load.wait()
@@ -283,15 +303,11 @@
         tail = jnp.concatenate(results, axis=-1).astype(jnp.bfloat16)
         tx_ref[p, :, 2 * feats :, :] = tail.reshape(n, feats, LANES)
 
-        @pl.when(p == 0)
-        def _():
-            send_to(0, n, p)
-
+        send_to(0, n, p)
         own(p).start()
         return carry
 
     lax.fori_loop(0, phases, phase, 0)
-    send_to(0, n, 1, 2)
 
     def drain(p, carry):
         whole(tx_ref, y_ref, b_send, b_recv, p).wait_recv()
@@ -361,6 +377,7 @@
                 dma((phases,)),
                 dma((10,)),
                 dma((phases,)),
+                pltpu.SemaphoreType.REGULAR,
                 dma((phases,)),
                 dma((phases,)),
                 dma((phases, 2)),

time: 134 us -> 130 us (0.970)
  Pallas kernels: 134 us -> 129 us
    pallas_call x1, Pallas kernels: 130 us -> 125 us  [body(): pl.pallas_call(functools.partial(kernel, n, phases), out_shape=jax.ShapeD...]
where the time goes in v4:
time: 130 us; the launch traced here: 129 us
  Pallas kernels  129 us (99%)
    pallas_call x1, Pallas kernels, body(): pl.pallas_call(functools.partial(kernel, n, phases), out_shape=jax.ShapeD...  125 us
    pallas_call x1, Pallas kernels, body(): pl.pallas_call(unpack, grid=(steps,), out_shape=jax.ShapeDtypeStruct((n,...  3.52 us

profile of v4, /device:TPU:431, one launch (start us, length us, event | category | flops | bytes accessed | tf_op | source)
XLA Modules:
  0.0 128.9 jit_solution(10796971155860837816)
XLA Ops:
  0.0 125.4 %shard_map.109.y_ref = bf16[3,32,24,128]{3,2,1,0:T(8,128)(2,1)} custom-call(bf16[32,3,2,8,192]{4,3,2,1,0:T(8,128)(2,1)} %bitcast.8, s32[8,192]{1,0:T(8,128)} %bitcast.10, s32[1,8]{1,0:T(1,128)} %bitcast.14, f32[64,192]{1,0:T(8,128)} %table_hbm.1, f32[1,192]{1,0:T(1,128)} %bitcast.11, f32[1,192]{1,0:T(1,128)} %bitcast.12, bf16[192,576]{1,0:T(8,128)(2,1)} %w_qkv_hbm.1, ...), custom_call_target="tpu_custom_call" | custom-call | tf_op jit(solution)/shard_map/pallas_call | solution.py:352
  125.4 3.5 %shard_map.110 = f32[32,3,2,8,192]{4,3,2,1,0:T(8,128)} custom-call(bf16[3,32,24,128]{3,2,1,0:T(8,128)(2,1)} %shard_map.109.y_ref), custom_call_target="tpu_custom_call" | custom-call | tf_op jit(solution)/shard_map/pallas_call | solution.py:403

commit v5 on v4

--- a/solution.py
+++ b/solution.py
@@ -267,11 +267,11 @@
 
         lane_head = lax.broadcasted_iota(jnp.int32, (half, width), 1) // head_dim
         results = []
-        for r in range(2):
-
-            def one_head(h, carry):
-                mine = lane_head == h
-                query = jnp.where(mine, q_ref[r].astype(jnp.float32), 0.0).astype(jnp.bfloat16)
+
+        def one_head(h, carry):
+            mine = lane_head == h
+            for r in range(2):
+                query = jnp.where(mine, q_ref[r], jnp.zeros_like(q_ref[r]))
                 scores = lax.dot_general(
                     query, k_ref[p, r], (((1,), (1,)), ((), ())), preferred_element_type=jnp.float32
                 )
@@ -281,12 +281,13 @@
                 got = jnp.dot(
                     probs.astype(jnp.bfloat16), v_ref[p, r], preferred_element_type=jnp.float32
                 )
-                ctx_ref[...] = jnp.where(mine, got.astype(jnp.bfloat16), ctx_ref[...])
-                return carry
-
-            lax.fori_loop(0, HEADS, one_head, 0)
+                ctx_ref[r] = jnp.where(mine, got, ctx_ref[r])
+            return carry
+
+        lax.fori_loop(0, HEADS, one_head, 0)
+        for r in range(2):
             mid = base_of(p, r) + jnp.dot(
-                ctx_ref[...], w_out_ref[...], preferred_element_type=jnp.float32
+                ctx_ref[r].astype(jnp.bfloat16), w_out_ref[...], preferred_element_type=jnp.float32
             )
             normed = cell_norm(mid, gain_two_ref[...]).astype(jnp.bfloat16)
             act = gelu(jnp.dot(normed, w_up_ref[...], preferred_element_type=jnp.float32))
@@ -303,11 +304,16 @@
         tail = jnp.concatenate(results, axis=-1).astype(jnp.bfloat16)
         tx_ref[p, :, 2 * feats :, :] = tail.reshape(n, feats, LANES)
 
-        send_to(0, n, p)
+
+        @pl.when(p == 0)
+        def _():
+            send_to(0, n, p)
+
         own(p).start()
         return carry
 
     lax.fori_loop(0, phases, phase, 0)
+    send_to(0, n, 1, 2)
 
     def drain(p, carry):
         whole(tx_ref, y_ref, b_send, b_recv, p).wait_recv()
@@ -373,7 +379,7 @@
                 vmem((2, half, width), jnp.bfloat16),
                 keys,
                 keys,
-                vmem((half, width), jnp.bfloat16),
+                vmem((2, half, width), jnp.float32),
                 dma((phases,)),
                 dma((10,)),
                 dma((phases,)),
@@ -399,7 +405,7 @@
             w_up,
             w_down.T,
         )
-        steps = 4 if n % 4 == 0 else 1
+        steps = 2
         out = pl.pallas_call(
             unpack,
             grid=(steps,),

time: 130 us -> 127 us (0.977)
  Pallas kernels: 129 us -> 127 us
where the time goes in v5:
time: 127 us
  Pallas kernels  127 us (100%)
    pallas_call x1, Pallas kernels, body(): pl.pallas_call(functools.partial(kernel, n, phases), out_shape=jax.ShapeD...  125 us

profile of v5, /device:TPU:431, one launch (start us, length us, event | category | flops | bytes accessed | tf_op | source)
XLA Modules:
  0.0 127.0 jit_solution(8132919807734853133)
XLA Ops:
  0.0 124.7 %shard_map.109.y_ref = bf16[3,32,24,128]{3,2,1,0:T(8,128)(2,1)} custom-call(bf16[32,3,2,8,192]{4,3,2,1,0:T(8,128)(2,1)} %bitcast.8, s32[8,192]{1,0:T(8,128)} %bitcast.10, s32[1,8]{1,0:T(1,128)} %bitcast.14, f32[64,192]{1,0:T(8,128)} %table_hbm.1, f32[1,192]{1,0:T(1,128)} %bitcast.11, f32[1,192]{1,0:T(1,128)} %bitcast.12, bf16[192,576]{1,0:T(8,128)(2,1)} %w_qkv_hbm.1, ...), custom_call_target="tpu_custom_call" | custom-call | tf_op jit(solution)/shard_map/pallas_call | solution.py:358
  124.7 2.2 %shard_map.110 = f32[32,3,2,8,192]{4,3,2,1,0:T(8,128)} custom-call(bf16[3,32,24,128]{3,2,1,0:T(8,128)(2,1)} %shard_map.109.y_ref), custom_call_target="tpu_custom_call" | custom-call | tf_op jit(solution)/shard_map/pallas_call | solution.py:409

commit v6 on v5

--- a/solution.py
+++ b/solution.py
@@ -284,7 +284,7 @@
                 ctx_ref[r] = jnp.where(mine, got, ctx_ref[r])
             return carry
 
-        lax.fori_loop(0, HEADS, one_head, 0)
+        lax.fori_loop(0, HEADS, one_head, 0, unroll=2)
         for r in range(2):
             mid = base_of(p, r) + jnp.dot(
                 ctx_ref[r].astype(jnp.bfloat16), w_out_ref[...], preferred_element_type=jnp.float32

time: 127 us -> 126 us (level)
  Pallas kernels: 127 us -> 125 us
    pallas_call x1, Pallas kernels: 125 us -> 123 us  [body(): pl.pallas_call(functools.partial(kernel, n, phases), out_shape=jax.ShapeD...]
where the time goes in v6:
time: 126 us; the launch traced here: 125 us
  Pallas kernels  125 us (99%)
    pallas_call x1, Pallas kernels, body(): pl.pallas_call(functools.partial(kernel, n, phases), out_shape=jax.ShapeD...  123 us

profile of v6, /device:TPU:431, one launch (start us, length us, event | category | flops | bytes accessed | tf_op | source)
XLA Modules:
  0.0 125.2 jit_solution(1288854891273032047)
XLA Ops:
  0.0 122.9 %shard_map.109.y_ref = bf16[3,32,24,128]{3,2,1,0:T(8,128)(2,1)} custom-call(bf16[32,3,2,8,192]{4,3,2,1,0:T(8,128)(2,1)} %bitcast.8, s32[8,192]{1,0:T(8,128)} %bitcast.10, s32[1,8]{1,0:T(1,128)} %bitcast.14, f32[64,192]{1,0:T(8,128)} %table_hbm.1, f32[1,192]{1,0:T(1,128)} %bitcast.11, f32[1,192]{1,0:T(1,128)} %bitcast.12, bf16[192,576]{1,0:T(8,128)(2,1)} %w_qkv_hbm.1, ...), custom_call_target="tpu_custom_call" | custom-call | tf_op jit(solution)/shard_map/pallas_call | solution.py:358
  122.9 2.2 %shard_map.110 = f32[32,3,2,8,192]{4,3,2,1,0:T(8,128)} custom-call(bf16[3,32,24,128]{3,2,1,0:T(8,128)(2,1)} %shard_map.109.y_ref), custom_call_target="tpu_custom_call" | custom-call | tf_op jit(solution)/shard_map/pallas_call | solution.py:409
